TPU v7x, 32 devices: a whole 2x2x4 slice. The times are simulated.
32 devices in a mesh: dp: 2 (over x), m1: 4 (over z), m2: 4 (over y, core).
Axes of the slice: x: 2, y: 2, z: 4, core: 2. Of those that a mesh axis runs over, the one named last changes fastest.
Arguments:
- x: bfloat16 [16, 256, 6144], P('dp', None, 'm1'), parts along dimension 0
- ln_scale: float32 [6144], replicated
- qn_scale: float32 [128], replicated
- kn_scale: float32 [128], replicated
- w_qkv: bfloat16 [6144, 3, 6144], P('m1', None, 'm2')
- w_up: bfloat16 [6144, 24576], P('m1', 'm2')
- b_up: float32 [24576], P('m2')
- w_o: bfloat16 [6144, 6144], P('m2', 'm1')
- w_down: bfloat16 [24576, 6144], P('m2', 'm1')
- b_out: float32 [6144], P('m1')
Outputs:
- output: bfloat16 [16, 256, 6144], P('dp', None, 'm1'), parts along dimension 0
There are 2 independent parts. A program takes and returns all parts, laid end to end along the dimension named above; an argument that names none is the same for every part.
All inputs are finite; a program needn't handle non-finite values.
Results may differ from a plain program's by a relative error of at most 0.0107519.
Values are sent between devices in bfloat16 or wider.
A program may use at most 1 GiB of HBM per device.

v0:
```python
import jax
import jax.numpy as jnp
from jax import lax
from jax.sharding import PartitionSpec as P

LN_EPS = 1e-6


def layer_norm(values, scale):
    mean = jnp.mean(values, axis=-1, keepdims=True)
    centered = values - mean
    variance = jnp.mean(centered * centered, axis=-1, keepdims=True)
    return centered * lax.rsqrt(variance + LN_EPS) * scale


def solution(mesh):
    group_m1 = mesh.shape['m1']

    def local_layer(x_blk, ln_scale, qn_scale, kn_scale, w_qkv, w_up, b_up, w_o, w_down, b_out):
        batch, patches, dim_local = x_blk.shape
        model_dim = dim_local * group_m1
        head_dim = qn_scale.shape[0]
        heads_local = w_qkv.shape[2] // head_dim
        scale_local = lax.dynamic_slice_in_dim(ln_scale, lax.axis_index('m1') * dim_local, dim_local)
        x_wide = x_blk.astype(jnp.float32)
        moments = jnp.stack([jnp.sum(x_wide, axis=-1), jnp.sum(x_wide * x_wide, axis=-1)])
        moments = lax.psum(moments, 'm1')
        mean = moments[0][..., None] / model_dim
        variance = moments[1][..., None] / model_dim - mean * mean
        normed = ((x_wide - mean) * lax.rsqrt(variance + LN_EPS) * scale_local).astype(jnp.bfloat16)
        qkv_part = jnp.einsum('bnd,dtc->bntc', normed, w_qkv, preferred_element_type=jnp.float32).astype(jnp.bfloat16)
        up_part = jnp.einsum('bnd,df->bnf', normed, w_up, preferred_element_type=jnp.float32).astype(jnp.bfloat16)
        proj_qkv, up_in = lax.psum((qkv_part, up_part), 'm1')
        proj_qkv = proj_qkv.reshape(batch, patches, 3, heads_local, head_dim)
        queries = layer_norm(proj_qkv[:, :, 0].astype(jnp.float32), qn_scale).astype(jnp.bfloat16)
        keys = layer_norm(proj_qkv[:, :, 1].astype(jnp.float32), kn_scale).astype(jnp.bfloat16)
        scores = jnp.einsum('bnhd,bmhd->bhnm', queries, keys, preferred_element_type=jnp.float32) * head_dim ** -0.5
        attn_probs = jax.nn.softmax(scores, axis=-1).astype(jnp.bfloat16)
        attended = jnp.einsum('bhnm,bmhd->bnhd', attn_probs, proj_qkv[:, :, 2], preferred_element_type=jnp.float32).astype(jnp.bfloat16)
        hidden = jax.nn.gelu(up_in.astype(jnp.float32) + b_up, approximate=False).astype(jnp.bfloat16)
        out_part = jnp.einsum('bnhd,hde->bne', attended, w_o.reshape(heads_local, head_dim, dim_local), preferred_element_type=jnp.float32)
        out_part = out_part + jnp.einsum('bnf,fe->bne', hidden, w_down, preferred_element_type=jnp.float32)
        mixed_sum = lax.psum(out_part.astype(jnp.bfloat16), 'm2')
        return (x_wide + mixed_sum.astype(jnp.float32) + b_out).astype(jnp.bfloat16)

    return jax.shard_map(local_layer, mesh=mesh, in_specs=(P('dp', None, 'm1'), P(), P(), P(), P('m1', None, 'm2'), P('m1', 'm2'), P('m2'), P('m2', 'm1'), P('m2', 'm1'), P('m1')), out_specs=P('dp', None, 'm1'), check_vma=False)
```

profile of v0, /device:TPU:0, one launch (start us, length us, event | category | flops | bytes accessed | tf_op | source)
XLA Modules:
  0.0 1941.0 jit_solution(13030201764163590147)
XLA Ops:
  6.5 0.0 all-reduce.6.cloned.1.call-start
  6.5 4.6 convert_reduce_fusion
  11.2 20.5 %psum.28 = f32[2,8,256]{2,1,0:T(8,128)S(1)} all-reduce(f32[2,8,256]{2,1,0:T(8,128)S(1)} %pad_maximum_fusion), channel_id=1, replica_groups=mesh['dp'=2,'m1'=4,'m2'=4] {'m1'}, use_global_device_ids=true, to_apply=%region_2.0 | all-reduce | flops 4096 | bytes 32768 | tf_op jit(solution)/shard_map/psum | solution.py:27
  31.8 0.8 dynamic_slice.3
  32.6 39.2 %fusion.27 = bf16[8,256,3,1536]{3,1,2,0:T(8,128)(2,1)} fusion(bf16[1536,3,1536]{2,0,1:T(8,128)(2,1)} %param.14, bf16[8,256,1536]{2,1,0:T(8,128)(2,1)} %param.10, f32[1536]{0:T(1024)S(1)} %dynamic_slice.3, f32[8,256]{1,0:T(8,128)S(1)} %fusion.75, f32[8,256]{1,0:T(8,128)S(1)} %fusion.76), kind=kOutput, calls=%fused_computation.42 | convolution fusion | flops 29016195072 | bytes 39344128 | tf_op jit(solution)/shard_map/bnd,dtc->bntc/dot_general | solution.py:31
  71.7 24.7 %copy.12 = bf16[8,256,3,1536]{1,3,2,0:T(8,128)(2,1)} copy(bf16[8,256,3,1536]{3,1,2,0:T(8,128)(2,1)} %fusion.27) | data formatting | bytes 37748736 | tf_op jit(solution)/shard_map/convert_element_type | solution.py:31
  96.4 48.1 %fusion.20 = bf16[8,256,6144]{2,1,0:T(8,128)(2,1)} fusion(bf16[1536,6144]{1,0:T(8,128)(2,1)} %param.15, bf16[8,256,1536]{2,1,0:T(8,128)(2,1)} %param.10, f32[1536]{0:T(1024)S(1)} %dynamic_slice.3, f32[8,256]{1,0:T(8,128)S(1)} %fusion.75, f32[8,256]{1,0:T(8,128)S(1)} %fusion.76), kind=kOutput, calls=%fused_computation.35 | convolution fusion | flops 38683017216 | bytes 50354176 | tf_op jit(solution)/shard_map/bnd,df->bnf/dot_general | solution.py:32
  144.6 0.0 copy-start.1
  144.6 0.0 copy-start.2
  144.6 0.0 all-reduce.6.cloned.1.call-update
  144.6 0.0 all-reduce.4.cloned.1.call-start
  144.7 1435.3 %all-reduce.6.cloned.1.call-done = (bf16[8,256,3,12,128]{1,4,3,2,0:T(8,128)(2,1)}, bf16[8,256,6144]{2,1,0:T(8,128)(2,1)}) async-done(((bf16[8,256,3,12,128]{1,4,3,2,0:T(8,128)(2,1)}, bf16[8,256,6144]{2,1,0:T(8,128)(2,1)}), (bf16[8,256,3,12,128]{1,4,3,2,0:T(8,128)(2,1)}, bf16[8,256,6144]{2,1,0:T(8,128)(2,1)})) %all-reduce.6.cloned.1.call-update) | async-done | bytes 44040208 | tf_op jit(solution)/shard_map/psum | solution.py:33
  1580.0 6.5 convert_reduce_fusion.2
  1586.5 7.4 fusion.33
  1594.0 0.0 copy-done.1
  1594.0 0.0 copy-done.2
  1594.0 13.8 fusion.55
  1607.9 27.1 %fusion.108 = (f32[8,12,256]{2,1,0:T(8,128)S(1)}, f32[8,12,256,256]{2,3,1,0:T(8,128)}) fusion(f32[8,12,256,256]{2,3,1,0:T(8,128)} %fusion.55), kind=kOutput, calls=%fused_computation.122 | output fusion | flops 25166080 | bytes 50429952 | tf_op jit(solution)/shard_map/sub | solution.py:38
  1634.9 0.0 copy-start.3
  1634.9 21.3 %fusion.59 = f32[8,256,1536,1]{2,1,3,0:T(8,128)} fusion(bf16[12,128,1536,1]{2,1,0,3:T(8,128)(2,1)} %bitcast.90, f32[8,12,256,256]{2,3,1,0:T(8,128)} %get-tuple-element.14, f32[8,12,256]{2,1,0:T(8,128)S(1)} %get-tuple-element.13, bf16[8,256,3,12,128]{1,4,3,2,0:T(8,128)(2,1)} %get-tuple-element.11), kind=kOutput, calls=%fused_computation.68 | convolution fusion | flops 11290017792 | bytes 48857088 | tf_op jit(solution)/shard_map/bnhd,hde->bne/dot_general | solution.py:41
  1656.3 0.0 copy-done.3
  1656.3 0.0 copy-start
  1656.3 149.7 %fusion.48 = bf16[8,256,1536]{2,1,0:T(8,128)(2,1)} fusion(f32[8,256,1536,1]{2,1,3,0:T(8,128)} %fusion.59, bf16[6144,1536]{1,0:T(8,128)(2,1)} %param.18, bf16[8,256,6144]{2,1,0:T(8,128)(2,1)} %get-tuple-element.12, f32[6144]{0:T(1024)S(1)} %copy-done.3), kind=kOutput, calls=%fused_computation.62 | convolution fusion | flops 39504052224 | bytes 62939136 | tf_op jit(solution)/shard_map/bnf,fe->bne/dot_general | solution.py:42
  1806.0 0.0 all-reduce.4.cloned.1.call-update
  1806.0 118.4 %all-reduce.4.cloned.1.call-done = bf16[8,256,1536]{2,1,0:T(8,128)(2,1)} async-done(((bf16[8,256,1536]{2,1,0:T(8,128)(2,1)}), bf16[8,256,1536]{2,1,0:T(8,128)(2,1)}) %all-reduce.4.cloned.1.call-update) | async-done | bytes 6291472 | tf_op jit(solution)/shard_map/psum | solution.py:43
  1924.4 0.0 copy-done
  1924.4 9.4 fusion.47
  (6 shorter events, 0.1 us)
Async XLA Ops:
  6.5 1573.4 %all-reduce.6.cloned.1.call-start = ((), (), s32[]{:S(2)}) async-start(), calls=%async_computation.1 | async-start | bytes 88080384 | tf_op jit(solution)/shard_map/psum | solution.py:33
  144.6 1449.4 %copy-start.1 = (f32[128]{0:T(128)S(1)}, f32[128]{0:T(128)}, u32[]{:S(2)}) copy-start(f32[128]{0:T(128)} %param.13) | copy-start | bytes 1540
  144.6 1449.4 %copy-start.2 = (f32[128]{0:T(128)S(1)}, f32[128]{0:T(128)}, u32[]{:S(2)}) copy-start(f32[128]{0:T(128)} %param.12) | copy-start | bytes 1540
  144.6 1779.8 %all-reduce.4.cloned.1.call-start = ((), (), s32[]{:S(2)}) async-start(), calls=%async_computation | async-start | bytes 12582912 | tf_op jit(solution)/shard_map/psum | solution.py:43
  1634.9 21.3 %copy-start.3 = (f32[6144]{0:T(1024)S(1)}, f32[6144]{0:T(1024)}, u32[]{:S(2)}) copy-start(f32[6144]{0:T(1024)} %param.16) | copy-start | bytes 73732
  1656.3 268.1 %copy-start = (f32[1536]{0:T(1024)S(1)}, f32[1536]{0:T(1024)}, u32[]{:S(2)}) copy-start(f32[1536]{0:T(1024)} %param.19) | copy-start | bytes 18436
Sparse Core Ops, SparseCore 0:
  144.7 1435.1 all-reduce.5
  1806.1 118.2 all-reduce.3
where the time goes:
time: 1960 us; the launch traced here: 1940 us
  waiting for transfers between devices  1550 us (79%)
  matrix products  272 us (14%)
  other arithmetic  55.2 us (3%)
  local copies, waits for them, and re-layouts  25.5 us (1%)
  blocking collectives  20.5 us (1%)
    psum x1, waiting for transfers between devices, local_layer(): proj_qkv, up_in = lax.psum((qkv_part, up_part), 'm1')  1440 us
    dot_general x1, matrix products, local_layer(): jnp.einsum('bnf,fe->bne', hidden, w_down, preferred_element_type=jnp.floa...  150 us
    psum x1, waiting for transfers between devices, local_layer(): mixed_sum = lax.psum(out_part.astype(jnp.bfloat16), 'm2')  118 us
    dot_general x1, matrix products, local_layer(): jnp.einsum('bnd,df->bnf', normed, w_up, preferred_element_type=jnp.float32)  48.1 us
  transfers between devices with their start and end apart: 2, of which 2 were waited for; matrix products, arithmetic and copies ran while one was open for 0% of the time, Pallas kernels for 0%

commit v1 on v0

v1 whole, which is shorter than its diff:
```python
import functools

import jax
import jax.numpy as jnp
from jax import lax
from jax.experimental import pallas as pl
from jax.experimental.pallas import tpu as pltpu
from jax.sharding import PartitionSpec as P

LN_EPS = 1e-6
MESH = pl.DeviceIdType.MESH
LANES = 128
LAG = 3


def xors(value):
    return (value, value + 1 - 2 * lax.rem(value, 2), value + 2 - 4 * lax.div(value, 2), 3 - value)


def ds(start, size):
    return pl.ds(pl.multiple_of(start, size if size < LANES else LANES), size)


def rows_at(start, size):
    return pl.ds(pl.multiple_of(start, 8), size)


def rcopy(src, dst, send_sem, recv_sem, device):
    return pltpu.make_async_remote_copy(src_ref=src, dst_ref=dst, send_sem=send_sem, recv_sem=recv_sem, device_id=device, device_id_type=MESH)


def dot(lhs, rhs):
    return jnp.dot(lhs, rhs, preferred_element_type=jnp.float32)


def head_norm(values, scale):
    mean = jnp.mean(values, axis=-1, keepdims=True)
    centered = values - mean
    variance = jnp.mean(centered * centered, axis=-1, keepdims=True)
    return (centered * lax.rsqrt(variance + LN_EPS) * scale).astype(jnp.bfloat16)


def kernel(sizes, x, lns, qns, kns, wq, wu, bu, wo, wd, bo,
           out, u, w1, w2, ra,
           xg, ubl, zq, h, rhs, lhs, w2b, pa, po, rav, ss, rb, rc, ud, rd, fin,
           xs, xr, w1s, w1r, f1s, f1r, us, ur, w2s, w2r, f2s, f2r,
           as_, ar, bs, br, cs, cr, dsm, drm, es, er, own_sem, rhs_sem, lhs_sem, ub_sem, w2b_sem, rav_sem, fin_sem):
    batch, patches, dim, qw, uw = sizes
    tokens = batch * patches
    rows = tokens // 4
    block = rows // 2
    half = dim // 2
    total = 4 * dim
    nub = uw // qw
    nc = dim // LANES
    wide = 4 * LANES
    heads = qw // LANES
    ln_rows = min(64, rows)

    g, i, j = lax.axis_index('dp'), lax.axis_index('m1'), lax.axis_index('m2')
    ip, jp = xors(i), xors(j)
    jy, jc = lax.div(j, 2), lax.rem(j, 2)

    barrier = pltpu.get_barrier_semaphore()
    peers = [{'m1': ip[e]} for e in (1, 2, 3)] + [{'m2': jp[e]} for e in (1, 2, 3)] + [{'dp': 1 - g}]
    for peer in peers:
        pl.semaphore_signal(barrier, inc=1, device_id=peer, device_id_type=MESH)
    pl.semaphore_wait(barrier, len(peers))

    mine = rows_at(j * rows, rows)
    x_far = rcopy(x.at[mine, :], xg.at[i], xs.at[0], xr.at[0], {'m1': ip[2]})
    x_near = rcopy(x.at[mine, :], xg.at[i], xs.at[1], xr.at[1], {'m1': ip[1]})
    x_own = pltpu.make_async_copy(x.at[mine, :], xg.at[i], own_sem.at[0])
    x_far.start()
    x_near.start()
    x_own.start()
    x_far_in = rcopy(xg.at[ip[2]], xg.at[ip[2]], xs.at[0], xr.at[0], {'m1': ip[2]})
    x_far_in.wait_recv()
    x_fwd = rcopy(xg.at[ip[2]], xg.at[ip[2]], xs.at[2], xr.at[2], {'m1': ip[1]})
    x_fwd.start()

    def z1(b, e):
        t = ip[e]
        if b < 3:
            src = wq.at[b, rows_at(g * half, half), ds(t * qw, qw)]
        else:
            src = wu.at[rows_at(g * half, half), ds(t * uw + (b - 3) * qw, qw)]
        return rcopy(src, w1.at[b, rows_at(i * dim + g * half, half), :], w1s.at[b, e - 1], w1r.at[b, e - 1], {'m1': t})

    def f1(b, e):
        part = w1.at[b, rows_at(ip[e] * dim + g * half, half), :]
        return rcopy(part, part, f1s.at[b, e - 1], f1r.at[b, e - 1], {'dp': 1 - g})

    def z1_in(b, e):
        part = w1.at[b, rows_at(ip[e] * dim + g * half, half), :]
        return rcopy(part, part, w1s.at[b, e - 1], w1r.at[b, e - 1], {'m1': ip[e]})

    def f1_in(b, e):
        part = w1.at[b, rows_at(ip[e] * dim + (1 - g) * half, half), :]
        return rcopy(part, part, f1s.at[b, e - 1], f1r.at[b, e - 1], {'dp': 1 - g})

    def forward1(b):
        for e in (2, 3, 1):
            z1_in(b, e).wait_recv()
            f1(b, e).start()

    for b in range(3 + nub):
        for e in (2, 3, 1):
            z1(b, e).start()

    def parts2(c, e, group, kind):
        size, first = (qw // 2, 0) if kind == 0 else (uw // 2, qw)
        return size, first + group * size

    def z2(c, e, kind):
        size, at = parts2(c, e, g, kind)
        t = ip[e]
        src = wo if kind == 0 else wd
        start = t * (2 * size) + g * size
        return rcopy(src.at[rows_at(start, size), ds(c * LANES, LANES)], w2.at[c, rows_at(at, size), ds(i * LANES, LANES)],
                     w2s.at[c, e - 1, kind], w2r.at[c, e - 1, kind], {'m1': t})

    def region2(c, e, group, kind):
        size, at = parts2(c, e, group, kind)
        return w2.at[c, rows_at(at, size), ds(ip[e] * LANES, LANES)]

    def z2_in(c, e, kind):
        part = region2(c, e, g, kind)
        return rcopy(part, part, w2s.at[c, e - 1, kind], w2r.at[c, e - 1, kind], {'m1': ip[e]})

    def f2(c, e, kind):
        part = region2(c, e, g, kind)
        return rcopy(part, part, f2s.at[c, e - 1, kind], f2r.at[c, e - 1, kind], {'dp': 1 - g})

    def f2_in(c, e, kind):
        part = region2(c, e, 1 - g, kind)
        return rcopy(part, part, f2s.at[c, e - 1, kind], f2r.at[c, e - 1, kind], {'dp': 1 - g})

    pieces2 = [(e, kind) for e in (2, 3, 1) for kind in (1, 0)]

    def issue2(first, last):
        @pl.loop(first, last)
        def _(c):
            for e, kind in pieces2:
                z2(c, e, kind).start()

    def forward2(c):
        for e, kind in pieces2:
            z2_in(c, e, kind).wait_recv()
            f2(c, e, kind).start()

    cuts = [nc * k // 4 for k in range(5)]

    x_own.wait()
    rcopy(xg.at[ip[1]], xg.at[ip[1]], xs.at[1], xr.at[1], {'m1': ip[1]}).wait_recv()
    rcopy(xg.at[ip[3]], xg.at[ip[3]], xs.at[2], xr.at[2], {'m1': ip[1]}).wait_recv()

    def u_out(r, slot):
        return pltpu.make_async_copy(ubl.at[slot], u.at[rows_at(j * rows + r * ln_rows, ln_rows), :], ub_sem.at[slot])

    @pl.loop(0, rows // ln_rows)
    def _(r):
        slot = lax.rem(r, 2)

        @pl.when(r >= 2)
        def _():
            u_out(r - 2, slot).wait()
        at = rows_at(r * ln_rows, ln_rows)
        parts = [xg[s, at, :].astype(jnp.float32) for s in range(4)]
        mean = sum(jnp.sum(part, axis=-1, keepdims=True) for part in parts) / total
        parts = [part - mean for part in parts]
        variance = sum(jnp.sum(part * part, axis=-1, keepdims=True) for part in parts) / total
        inverse = lax.rsqrt(variance + LN_EPS)
        for s in range(4):
            cols = slice(s * dim, (s + 1) * dim)
            ubl[slot, :, cols] = (parts[s] * inverse * lns[:, cols]).astype(jnp.bfloat16)
        u_out(r, slot).start()

    for r in range(max(0, rows // ln_rows - 2), rows // ln_rows):
        u_out(r, r % 2).wait()

    def u_rows(q):
        return u.at[rows_at(q * rows, rows), :]

    u_far = rcopy(u_rows(j), u_rows(j), us.at[0], ur.at[0], {'m2': jp[2]})
    u_near = rcopy(u_rows(j), u_rows(j), us.at[1], ur.at[1], {'m2': jp[1]})
    u_far.start()
    u_near.start()
    for b in range(4):
        forward1(b)
    issue2(cuts[0], cuts[1])
    rcopy(u_rows(jp[2]), u_rows(jp[2]), us.at[0], ur.at[0], {'m2': jp[2]}).wait_recv()
    u_fwd = rcopy(u_rows(jp[2]), u_rows(jp[2]), us.at[2], ur.at[2], {'m2': jp[1]})
    u_fwd.start()
    rcopy(u_rows(jp[1]), u_rows(jp[1]), us.at[1], ur.at[1], {'m2': jp[1]}).wait_recv()
    rcopy(u_rows(jp[3]), u_rows(jp[3]), us.at[2], ur.at[2], {'m2': jp[1]}).wait_recv()

    def lhs_in(m, slot):
        return pltpu.make_async_copy(u.at[rows_at(m * block, block), :], lhs.at[slot], lhs_sem.at[slot])

    def product1(b, own, store):
        for e in (1, 2, 3):
            f1_in(b, e).wait_recv()
        loads = [pltpu.make_async_copy(own, rhs.at[rows_at(i * dim, dim), :], rhs_sem.at[0])]
        for e in (1, 2, 3):
            at = rows_at(ip[e] * dim, dim)
            loads.append(pltpu.make_async_copy(w1.at[b, at, :], rhs.at[at, :], rhs_sem.at[e]))
        for load in loads:
            load.start()
        lhs_in(0, 0).start()
        for load in loads:
            load.wait()

        @pl.loop(0, tokens // block)
        def _(m):
            slot = lax.rem(m, 2)
            lhs_in(m, slot).wait()

            @pl.when(m + 1 < tokens // block)
            def _():
                lhs_in(m + 1, 1 - slot).start()
            store(rows_at(m * block, block), dot(lhs[slot], rhs[...]))

    @pl.loop(0, 3)
    def _(b):
        def store(at, value):
            zq[b, at, :] = value.astype(jnp.bfloat16)
        product1(b, wq.at[b, :, ds(i * qw, qw)], store)

    forward1(4)
    issue2(cuts[1], cuts[2])

    @pl.loop(0, batch)
    def _(n):
        at = rows_at(n * patches, patches)
        for head in range(heads):
            cols = slice(head * LANES, (head + 1) * LANES)
            query = head_norm(zq[0, at, cols].astype(jnp.float32), qns[...])
            key = head_norm(zq[1, at, cols].astype(jnp.float32), kns[...])
            scores = lax.dot_general(query, key, (((1,), (1,)), ((), ())), preferred_element_type=jnp.float32) * LANES ** -0.5
            scores = jnp.exp(scores - jnp.max(scores, axis=-1, keepdims=True))
            probs = (scores / jnp.sum(scores, axis=-1, keepdims=True)).astype(jnp.bfloat16)
            h[at, cols] = dot(probs, zq[2, at, cols]).astype(jnp.bfloat16)

    forward1(5)
    issue2(cuts[2], cuts[3])

    @pl.loop(0, nub)
    def _(b):
        def store(at, value):
            value = value.astype(jnp.bfloat16).astype(jnp.float32) + bu[:, ds(i * uw + b * qw, qw)]
            value = 0.5 * value * (1.0 + lax.erf(value * 2.0 ** -0.5))
            h[at, ds(qw + b * qw, qw)] = value.astype(jnp.bfloat16)
        product1(b + 3, wu.at[:, ds(i * uw + b * qw, qw)], store)

        @pl.when(b == 1)
        def _():
            forward1(6)
            issue2(cuts[3], cuts[4])

    def quarter(yy, core):
        return (2 * yy + core) * rows

    def send_a(c, yy):
        return rcopy(pa.at[lax.rem(c, 2), yy], ra.at[c, yy], as_.at[c, yy], ar.at[c, yy], {'m2': jp[1]})

    def send_b(c):
        return rcopy(ss.at[lax.rem(c, 2)], rb.at[c], bs.at[c], br.at[c], {'m2': jp[2]})

    def send_c(c, k):
        src = rb.at[c, :, ds(ip[1 + 2 * k] * LANES, LANES)]
        return rcopy(src, rc.at[c, k], cs.at[c, k], cr.at[c, k], {'m1': ip[1]})

    def send_d(c):
        return rcopy(ud.at[c], rd.at[c], dsm.at[c], drm.at[c], {'m1': ip[2]})

    def out_part(c, q):
        return out.at[rows_at(q * rows, rows), ds(c * LANES, LANES)]

    def send_e(c, e):
        return rcopy(fin.at[c], out_part(c, j), es.at[c, e - 1], er.at[c, e - 1], {'m2': jp[e]})

    def out_own(c):
        return pltpu.make_async_copy(fin.at[c], out_part(c, j), fin_sem.at[c])

    forward2(0)

    @pl.loop(0, nc + 2)
    def _(c):
        @pl.when(c + 1 < nc)
        def _():
            forward2(c + 1)

        @pl.when(c < nc)
        def _():
            slot = lax.rem(c, 2)
            for e, kind in pieces2:
                f2_in(c, e, kind).wait_recv()
            cols = ds(i * LANES, LANES)
            loads = [pltpu.make_async_copy(wo.at[rows_at(i * qw, qw), ds(c * LANES, LANES)], w2b.at[slot, 0:qw, cols], w2b_sem.at[0]),
                     pltpu.make_async_copy(wd.at[rows_at(i * uw, uw), ds(c * LANES, LANES)], w2b.at[slot, qw:qw + uw, cols], w2b_sem.at[4])]
            for e in (1, 2, 3):
                cols = ds(ip[e] * LANES, LANES)
                loads.append(pltpu.make_async_copy(w2.at[c, :, cols], w2b.at[slot, :, cols], w2b_sem.at[e]))
            for load in loads:
                load.start()

            @pl.when(c >= 2)
            def _():
                for yy in range(2):
                    send_a(c - 2, yy).wait_send()
            for load in loads:
                load.wait()
            for yy in range(2):
                for sub in range(2):
                    at = rows_at(quarter(yy, 1 - jc) + sub * block, block)
                    pa[slot, yy, sub * block:(sub + 1) * block, :] = dot(h[at, :], w2b[slot]).astype(jnp.bfloat16)
                send_a(c, yy).start()
            keep = lax.rem(c, 3)
            for yy in range(2):
                for sub in range(2):
                    at = rows_at(quarter(yy, jc) + sub * block, block)
                    po[keep, yy, sub * block:(sub + 1) * block, :] = dot(h[at, :], w2b[slot]).astype(jnp.bfloat16)

        @pl.when((c >= 1) & (c <= nc))
        def _():
            d = c - 1
            keep = lax.rem(d, 3)
            for yy in range(2):
                part = ra.at[d, yy]
                rcopy(part, part, as_.at[d, yy], ar.at[d, yy], {'m2': jp[1]}).wait_recv()
            load = pltpu.make_async_copy(ra.at[d], rav, rav_sem.at[0])
            load.start()

            @pl.when(d >= 2)
            def _():
                send_b(d - 2).wait_send()
            load.wait()
            ss[lax.rem(d, 2)] = (po[keep, 1 - jy].astype(jnp.float32) + rav[1 - jy].astype(jnp.float32)).astype(jnp.bfloat16)
            send_b(d).start()
            po[keep, jy] = (po[keep, jy].astype(jnp.float32) + rav[jy].astype(jnp.float32)).astype(jnp.bfloat16)

        @pl.when(c >= 2)
        def _():
            d = c - 2
            rcopy(rb.at[d], rb.at[d], bs.at[d], br.at[d], {'m2': jp[2]}).wait_recv()
            rb[d] = (po[lax.rem(d, 3), jy].astype(jnp.float32) + rb[d].astype(jnp.float32)).astype(jnp.bfloat16)
            for k in range(2):
                send_c(d, k).start()

    @pl.loop(0, nc + LAG)
    def _(c):
        @pl.when(c < nc)
        def _():
            for k in range(2):
                rcopy(rc.at[c, k], rc.at[c, k], cs.at[c, k], cr.at[c, k], {'m1': ip[1]}).wait_recv()
            far = rb[c, :, ds(ip[2] * LANES, LANES)].astype(jnp.float32) + rc[c, 1].astype(jnp.float32)
            ud[c] = far.astype(jnp.bfloat16)
            send_d(c).start()

        @pl.when(c >= LAG)
        def _():
            d = c - LAG
            rcopy(rd.at[d], rd.at[d], dsm.at[d], drm.at[d], {'m1': ip[2]}).wait_recv()
            cols = ds(d * LANES, LANES)
            value = rb[d, :, ds(i * LANES, LANES)].astype(jnp.float32) + rc[d, 0].astype(jnp.float32) + rd[d].astype(jnp.float32)
            value = xg[i, :, cols].astype(jnp.float32) + value + bo[:, cols]
            fin[d] = value.astype(jnp.bfloat16)
            for e in (2, 3, 1):
                send_e(d, e).start()
            out_own(d).start()

    for copy in (x_far, x_near, x_fwd, u_far, u_near, u_fwd):
        copy.wait_send()
    for b in range(3 + nub):
        for e in (2, 3, 1):
            z1(b, e).wait_send()
            f1(b, e).wait_send()

    @pl.loop(0, nc)
    def _(c):
        for e, kind in pieces2:
            z2(c, e, kind).wait_send()
            f2(c, e, kind).wait_send()
        for k in range(2):
            send_c(c, k).wait_send()
        send_d(c).wait_send()
        out_own(c).wait()
        for e in (1, 2, 3):
            send_e(c, e).wait_send()
            part = out_part(c, jp[e])
            rcopy(part, part, es.at[c, e - 1], er.at[c, e - 1], {'m2': jp[e]}).wait_recv()

        @pl.when(c >= nc - 2)
        def _():
            for yy in range(2):
                send_a(c, yy).wait_send()
            send_b(c).wait_send()


def solution(mesh):
    assert mesh.shape['m1'] == 4 and mesh.shape['m2'] == 4 and mesh.shape['dp'] == 2

    def local_layer(x_blk, ln_scale, qn_scale, kn_scale, w_qkv, w_up, b_up, w_o, w_down, b_out):
        batch, patches, dim = x_blk.shape
        tokens = batch * patches
        qw, uw = w_qkv.shape[2] // 4, w_up.shape[1] // 4
        rows, block, nc, nb = tokens // 4, tokens // 8, dim // LANES, 3 + uw // qw
        assert qn_scale.shape[0] == LANES and uw % qw == 0 and nb == 7
        wide = 4 * LANES
        bf16 = jnp.bfloat16
        dma = pltpu.SemaphoreType.DMA
        hbm = pl.BlockSpec(memory_space=pltpu.HBM)
        vmem = pl.BlockSpec(memory_space=pltpu.VMEM)
        ln_rows = min(64, rows)
        out = pl.pallas_call(
            functools.partial(kernel, (batch, patches, dim, qw, uw)),
            out_shape=[
                jax.ShapeDtypeStruct((tokens, dim), bf16),
                jax.ShapeDtypeStruct((tokens, 4 * dim), bf16),
                jax.ShapeDtypeStruct((nb, 4 * dim, qw), bf16),
                jax.ShapeDtypeStruct((nc, qw + uw, wide), bf16),
                jax.ShapeDtypeStruct((nc, 2, rows, wide), bf16)],
            in_specs=[hbm, vmem, vmem, vmem, hbm, hbm, vmem, hbm, hbm, vmem],
            out_specs=[hbm] * 5,
            scratch_shapes=[
                pltpu.VMEM((4, rows, dim), bf16),
                pltpu.VMEM((2, ln_rows, 4 * dim), bf16),
                pltpu.VMEM((3, tokens, qw), bf16),
                pltpu.VMEM((tokens, qw + uw), bf16),
                pltpu.VMEM((4 * dim, qw), bf16),
                pltpu.VMEM((2, block, 4 * dim), bf16),
                pltpu.VMEM((2, qw + uw, wide), bf16),
                pltpu.VMEM((2, 2, rows, wide), bf16),
                pltpu.VMEM((3, 2, rows, wide), bf16),
                pltpu.VMEM((2, rows, wide), bf16),
                pltpu.VMEM((2, rows, wide), bf16),
                pltpu.VMEM((nc, rows, wide), bf16),
                pltpu.VMEM((nc, 2, rows, LANES), bf16),
                pltpu.VMEM((nc, rows, LANES), bf16),
                pltpu.VMEM((nc, rows, LANES), bf16),
                pltpu.VMEM((nc, rows, LANES), bf16),
                dma((3,)), dma((3,)),
                dma((nb, 3)), dma((nb, 3)), dma((nb, 3)), dma((nb, 3)),
                dma((3,)), dma((3,)),
                dma((nc, 3, 2)), dma((nc, 3, 2)), dma((nc, 3, 2)), dma((nc, 3, 2)),
                dma((nc, 2)), dma((nc, 2)), dma((nc,)), dma((nc,)), dma((nc, 2)), dma((nc, 2)), dma((nc,)), dma((nc,)),
                dma((nc, 3)), dma((nc, 3)),
                dma((1,)), dma((4,)), dma((2,)), dma((2,)), dma((5,)), dma((1,)), dma((nc,))],
            compiler_params=pltpu.CompilerParams(collective_id=0, has_side_effects=True, vmem_limit_bytes=67_043_328),
            name='layer',
        )(x_blk.reshape(tokens, dim), ln_scale[None], qn_scale[None], kn_scale[None], w_qkv.transpose(1, 0, 2), w_up,
          b_up_all(b_up), w_o, w_down, b_out[None])[0]
        return out.reshape(batch, patches, dim)

    def b_up_all(b_up):
        return b_up[None]

    return jax.shard_map(local_layer, mesh=mesh, in_specs=(P('dp', None, 'm1'), P(), P(), P(), P('m1', None, 'm2'), P('m1', 'm2'), P('m2'), P('m2', 'm1'), P('m2', 'm1'), P('m1')), out_specs=P('dp', None, 'm1'), check_vma=False)
```

time: 1960 us -> 894 us (0.46)
  waiting for transfers between devices: 1550 us -> 0 us
  Pallas kernels: 0 us -> 884 us
  matrix products: 272 us -> 0 us
  other arithmetic: 55.2 us -> 0 us
  blocking collectives: 20.5 us -> 0 us
    psum x2 -> x0, waiting for transfers between devices: 1550 us -> none  [the longest x1 1440 us: local_layer(): proj_qkv, up_in = lax.psum((qkv_part, up_part), 'm1')]
    pallas_call x0 -> x1, Pallas kernels: none -> 884 us  [local_layer(): pl.pallas_call(functools.partial(kernel, (batch, patches, dim, qw, uw)),...]
    dot_general x5 -> x0, matrix products: 272 us -> none  [the longest x1 150 us: local_layer(): jnp.einsum('bnf,fe->bne', hidden, w_down, preferred_element_type=jnp.floa...]
    sub x1 -> x0, other arithmetic: 27.1 us -> none  [local_layer(): attn_probs = jax.nn.softmax(scores, axis=-1).astype(jnp.bfloat16)]
    convert_element_type x1 -> x0, local copies, waits for them, and re-layouts: 24.7 us -> none  [local_layer(): jnp.einsum('bnd,dtc->bntc', normed, w_qkv, preferred_element_type=jnp.flo...]
    psum x1 -> x0, blocking collectives: 20.5 us -> none  [local_layer(): moments = lax.psum(moments, 'm1')]
  transfers between devices with their start and end apart: 2 -> 0, of which waited for: 2 -> 0; matrix products, arithmetic and copies ran while one was open for 0% -> 0% of each run, Pallas kernels for 0% -> 0%
where the time goes in v1:
time: 894 us; the launch traced here: 891 us
  Pallas kernels  884 us (99%)
    pallas_call x1, Pallas kernels, local_layer(): pl.pallas_call(functools.partial(kernel, (batch, patches, dim, qw, uw)),...  884 us

profile of v1, /device:TPU:0, one launch (start us, length us, event | category | flops | bytes accessed | tf_op | source)
XLA Modules:
  0.0 890.8 jit_solution(9255068971156757868)
XLA Ops:
  0.0 1.3 broadcast_in_dim.19.bo
  1.3 883.6 %layer.1 = (bf16[2048,1536]{1,0:T(8,128)(2,1)}, bf16[2048,6144]{1,0:T(8,128)(2,1)}, bf16[7,6144,384]{2,1,0:T(8,128)(2,1)}, bf16[12,1920,512]{2,1,0:T(8,128)(2,1)}, bf16[12,2,512,512]{3,2,1,0:T(8,128)(2,1)}) custom-call(bf16[2048,1536]{1,0:T(8,128)(2,1)} %bitcast.9, f32[1,6144]{1,0:T(1,128)} %bitcast.10, f32[1,128]{1,0:T(1,128)} %bitcast.12, ...), custom_call_target="tpu_custom_call" | custom-call | tf_op jit(solution)/shard_map/layer/pallas_call | solution.py:416
  884.9 5.9 copy.12
